TPU v7x, 128 devices: a whole 4x4x4 slice. The times are simulated.
128 devices in a mesh: ep: 8 (over y, core), fs: 16 (over z, x).
Axes of the slice: x: 4, y: 4, z: 4, core: 2. Of those that a mesh axis runs over, the one named last changes fastest.
Arguments:
- grads: bfloat16 [8, 8, 256, 14336], P('ep', None, 'fs'), may hold values from -64 to 64
- counts: int32 [8, 8], replicated, may hold values from 16 to 2047
- weight: bfloat16 [8, 256, 14336], P('ep', 'fs'), may hold values from -3 to 3
- mom: float32 [8, 256, 14336], P('ep', 'fs'), may hold values from -64 to 64
- second: float32 [8, 256, 14336], P('ep', 'fs'), may hold values from 0.1 to 10
- in_weight: float32 [6, 32], replicated, may hold values from -2.5 to 2.5
- in_bias: float32 [32], replicated, may hold values from -3 to 3
- out_weight: float32 [32, 2], replicated, may hold values from -1 to 1
- out_bias: float32 [2], replicated, may hold values from -3 to 3
Outputs:
- new_weight: bfloat16 [8, 256, 14336], P('ep')
- new_mom: float32 [8, 256, 14336], P('ep', 'fs')
- new_second: float32 [8, 256, 14336], P('ep', 'fs')
All inputs are finite; a program needn't handle non-finite values.
Results may differ from a plain program's by a relative error of at most 0.0019.
Values may be sent and summed in bfloat16 or wider, within the bound.
A program may use at most 64 MiB of HBM per device.

v0:
```python
import jax
import jax.numpy as jnp
from jax import lax
from jax.sharding import PartitionSpec as P

MOMENTUM_DECAY = 0.9
SECOND_DECAY = 0.99
NORM_EPS = 1e-06
ROOT_EPS = 1e-08
STEP_SCALE = 0.2
EXP_SCALE = 0.5


def from_everyone(value, axis):
    copies = jnp.broadcast_to(value, (lax.axis_size(axis), *value.shape))
    return lax.all_to_all(copies, axis, split_axis=0, concat_axis=0, tiled=True)


def of_everyone(value, axis):
    return from_everyone(value, axis).sum(axis=0)


def in_one(arrays, axis):
    line, at, done = (jnp.concatenate([a.reshape(-1) for a in arrays]), 0, [])
    so_far = of_everyone(line, axis)
    for a in arrays:
        done.append(so_far[at : at + a.size].reshape(a.shape))
        at += a.size
    return tuple(done)


def learned_step(
    gradient,
    mom_next,
    second_next,
    weight,
    grad_norm,
    mom_norm,
    in_weight,
    in_bias,
    out_weight,
    out_bias,
):
    inv_root = lax.rsqrt(second_next + ROOT_EPS)
    features = jnp.stack(
        [
            gradient / grad_norm,
            mom_next / mom_norm,
            mom_next * inv_root,
            gradient * inv_root,
            weight.astype(jnp.float32),
            jnp.broadcast_to(jnp.log(mom_norm), gradient.shape),
        ]
    )
    hidden = jax.nn.relu(
        jnp.einsum("fh,fab->hab", in_weight, features, precision=lax.Precision.HIGHEST)
        + in_bias[:, None, None]
    )
    outputs = (
        jnp.einsum("hk,hab->kab", out_weight, hidden, precision=lax.Precision.HIGHEST)
        + out_bias[:, None, None]
    )
    update = STEP_SCALE * outputs[0] * jnp.exp(EXP_SCALE * outputs[1])
    return (weight.astype(jnp.float32) - update).astype(jnp.bfloat16)


def add_sources(arrived):
    return jnp.sum(arrived.astype(jnp.float32), axis=0)


def per_device(grads, counts, weight, mom, second, in_weight, in_bias, out_weight, out_bias):
    source = lax.axis_index("ep")
    counts_f = counts.astype(jnp.float32)
    totals = jnp.sum(counts_f, axis=0)
    share_row = lax.dynamic_index_in_dim(counts_f, source, 0, keepdims=False) / totals
    weighted = share_row[None, :, None, None] * grads.astype(jnp.float32)
    outgoing = weighted.astype(jnp.bfloat16)
    gradient = add_sources(lax.all_to_all(outgoing, "ep", split_axis=1, concat_axis=0, tiled=True))[
        0
    ]
    mom_here = mom[0]
    second_here = second[0]
    mom_next = MOMENTUM_DECAY * mom_here + (1.0 - MOMENTUM_DECAY) * gradient
    second_next = SECOND_DECAY * second_here + (1.0 - SECOND_DECAY) * gradient * gradient
    entries = gradient.shape[0] * gradient.shape[1] * lax.axis_size("fs")
    grad_sq, mom_sq = in_one((jnp.sum(gradient * gradient), jnp.sum(mom_next * mom_next)), "fs")
    grad_norm = jnp.sqrt(grad_sq / entries + NORM_EPS)
    mom_norm = jnp.sqrt(mom_sq / entries + NORM_EPS)
    width = gradient.shape[1]

    def block_step(items):
        grad_block, mom_block, second_block, weight_block = items
        return learned_step(
            grad_block,
            mom_block,
            second_block,
            weight_block,
            grad_norm,
            mom_norm,
            in_weight,
            in_bias,
            out_weight,
            out_bias,
        )

    blocks = lax.map(
        block_step,
        (
            gradient.reshape(-1, 2, width),
            mom_next.reshape(-1, 2, width),
            second_next.reshape(-1, 2, width),
            weight[0].reshape(-1, 2, width),
        ),
    )
    updated = blocks.reshape(gradient.shape)
    gathered = lax.all_gather(updated[None], "fs", axis=1, tiled=True)
    return (gathered, mom_next[None], second_next[None])


def solution(mesh):
    in_specs = (
        P("ep", None, "fs", None),
        P(),
        P("ep", "fs", None),
        P("ep", "fs", None),
        P("ep", "fs", None),
        P(),
        P(),
        P(),
        P(),
    )
    out_specs = (P("ep", None, None), P("ep", "fs", None), P("ep", "fs", None))
    return jax.shard_map(
        per_device, mesh=mesh, in_specs=in_specs, out_specs=out_specs, check_vma=False
    )
```

profile of v0, /device:TPU:1, one launch (start us, length us, event | category | flops | bytes accessed | tf_op | source)
XLA Modules:
  0.0 246.2 jit_solution(12678078749305325285)
XLA Ops:
  8.6 4.7 %multiply_convert_fusion = bf16[1,8,16,14336]{3,2,0,1:T(8,128)(2,1)} fusion(bf16[1,8,16,14336]{3,2,1,0:T(8,128)(2,1)} %param.11, f32[8]{0:T(128)S(1)} %bitcast_divide_fusion), kind=kLoop, calls=%fused_computation.22 | loop fusion | flops 5505024 | bytes 7340064 | tf_op jit(solution)/shard_map/convert_element_type | solution.py:77
  13.3 6.1 %all-to-all-start = ((bf16[1,8,16,14336]{3,2,0,1:T(8,128)(2,1)}), bf16[1,8,16,14336]{3,2,0,1:T(8,128)(2,1)}, u32[]{:S(2)}, u32[]{:S(2)}) async-start(bf16[1,8,16,14336]{3,2,0,1:T(8,128)(2,1)} %multiply_convert_fusion), calls=%async_computation | async-start | bytes 7340032 | tf_op jit(solution)/shard_map/all_to_all | solution.py:78
  19.7 42.8 %all-to-all-done = bf16[1,8,16,14336]{3,2,0,1:T(8,128)(2,1)} async-done(((bf16[1,8,16,14336]{3,2,0,1:T(8,128)(2,1)}), bf16[1,8,16,14336]{3,2,0,1:T(8,128)(2,1)}, u32[]{:S(2)}, u32[]{:S(2)}) %all-to-all-start) | async-done | bytes 3670048 | tf_op jit(solution)/shard_map/all_to_all | solution.py:78
  62.5 2.6 %convert_reduce_fusion = f32[16,14336]{1,0:T(8,128)S(1)} fusion(bf16[1,8,16,14336]{3,2,0,1:T(8,128)(2,1)} %all-to-all-done), kind=kLoop, calls=%fused_computation.21 | loop fusion | flops 3440640 | bytes 4587520 | tf_op jit(solution)/shard_map/reduce_sum | solution.py:68
  69.5 7.6 %all-to-all-start.1 = ((f32[16,1,2]{2,1,0:T(1,128)}), f32[16,1,2]{2,1,0:T(1,128)S(1)}, u32[]{:S(2)}, u32[]{:S(2)}) async-start(f32[16,1,2]{2,1,0:T(1,128)} %broadcast_in_dim.18), calls=%async_computation.1 | async-start | bytes 16384 | tf_op jit(solution)/shard_map/all_to_all | solution.py:16
  77.3 2.9 %fusion.10 = (f32[1,16,14336]{2,1,0:T(8,128)}, f32[1,16,14336]{2,1,0:T(8,128)}, f32[1,16,14336]{2,1,0:T(8,128)}, f32[1,16,14336]{2,1,0:T(8,128)S(1)}) fusion(f32[16,14336]{1,0:T(8,128)S(1)} %convert_reduce_fusion, f32[1,16,14336]{2,1,0:T(8,128)} %param.15, f32[1,16,14336]{2,1,0:T(8,128)S(1)} %copy-done), kind=kLoop, calls=%fused_computation.26 | loop fusion | flops 1605632 | bytes 6422528 | tf_op jit(solution)/shard_map/add | solution.py:84
  82.5 4.1 %fusion.9 = (f32[8,2,14336]{2,0,1:T(8,128)S(1)}, f32[8,2,14336]{2,0,1:T(8,128)}, f32[8,2,14336]{2,0,1:T(8,128)}) fusion(f32[8,2,14336]{2,1,0:T(2,128)S(1)} %mul.131, f32[8,2,14336]{2,1,0:T(2,128)} %reshape_squeeze.7, f32[8,2,14336]{2,1,0:T(2,128)S(1)} %mul.126), kind=kLoop, calls=%fused_computation.25 | loop fusion | flops 1146880 | bytes 5505024 | tf_op jit(solution)/shard_map/add | solution.py:84
  88.4 75.6 %while.11 = (s32[]{:T(128)}, bf16[8,2,14336]{2,1,0:T(2,128)(2,1)}, bf16[8,2,14336]{2,1,0:T(2,128)(2,1)S(1)}, f32[8,2,14336]{2,0,1:T(8,128)}, f32[]{:T(128)}, /*i...) while((s32[]{:T(128)}, bf16[8,2,14336]{2,1,0:T(2,128)(2,1)}, ...), condition=%wide.region_6.7_spmd, body=%wide.region_5.6_spmd.sunk | while | flops 90316800 | bytes 11298093 | solution.py:106
  88.7 1.8 dynamic-slice_multiply_fusion.3
  91.6 3.2 %fusion.28 = f32[32,2,14336]{2,0,1:T(8,128)S(1)} fusion(f32[6,2,14336]{2,0,1:T(8,128)S(1)} %stack.4, f32[32]{0:T(128)S(1)} %get-tuple-element.350, f32[6,32]{1,0:T(8,128)S(1)} %get-tuple-element.349), kind=kOutput, calls=%fused_computation.2.clone.1 | convolution fusion | flops 67895296 | bytes 4359040 | tf_op jit(solution)/shard_map/while/body/eval_jaxpr/fh,fab->hab/dot_general | solution.py:56
  94.8 2.1 fusion.29
  98.1 1.8 dynamic-slice_multiply_fusion.3
  101.1 3.2 %fusion.28 = f32[32,2,14336]{2,0,1:T(8,128)S(1)} fusion(f32[6,2,14336]{2,0,1:T(8,128)S(1)} %stack.4, f32[32]{0:T(128)S(1)} %get-tuple-element.350, f32[6,32]{1,0:T(8,128)S(1)} %get-tuple-element.349), kind=kOutput, calls=%fused_computation.2.clone.1 | convolution fusion | flops 67895296 | bytes 4359040 | tf_op jit(solution)/shard_map/while/body/eval_jaxpr/fh,fab->hab/dot_general | solution.py:56
  104.3 2.1 fusion.29
  107.6 1.8 dynamic-slice_multiply_fusion.3
  110.5 3.2 %fusion.28 = f32[32,2,14336]{2,0,1:T(8,128)S(1)} fusion(f32[6,2,14336]{2,0,1:T(8,128)S(1)} %stack.4, f32[32]{0:T(128)S(1)} %get-tuple-element.350, f32[6,32]{1,0:T(8,128)S(1)} %get-tuple-element.349), kind=kOutput, calls=%fused_computation.2.clone.1 | convolution fusion | flops 67895296 | bytes 4359040 | tf_op jit(solution)/shard_map/while/body/eval_jaxpr/fh,fab->hab/dot_general | solution.py:56
  113.7 2.1 fusion.29
  117.0 1.8 dynamic-slice_multiply_fusion.3
  120.0 3.2 %fusion.28 = f32[32,2,14336]{2,0,1:T(8,128)S(1)} fusion(f32[6,2,14336]{2,0,1:T(8,128)S(1)} %stack.4, f32[32]{0:T(128)S(1)} %get-tuple-element.350, f32[6,32]{1,0:T(8,128)S(1)} %get-tuple-element.349), kind=kOutput, calls=%fused_computation.2.clone.1 | convolution fusion | flops 67895296 | bytes 4359040 | tf_op jit(solution)/shard_map/while/body/eval_jaxpr/fh,fab->hab/dot_general | solution.py:56
  123.2 2.1 fusion.29
  126.4 1.8 dynamic-slice_multiply_fusion.3
  129.4 3.2 %fusion.28 = f32[32,2,14336]{2,0,1:T(8,128)S(1)} fusion(f32[6,2,14336]{2,0,1:T(8,128)S(1)} %stack.4, f32[32]{0:T(128)S(1)} %get-tuple-element.350, f32[6,32]{1,0:T(8,128)S(1)} %get-tuple-element.349), kind=kOutput, calls=%fused_computation.2.clone.1 | convolution fusion | flops 67895296 | bytes 4359040 | tf_op jit(solution)/shard_map/while/body/eval_jaxpr/fh,fab->hab/dot_general | solution.py:56
  132.6 2.1 fusion.29
  138.9 3.2 %fusion.28 = f32[32,2,14336]{2,0,1:T(8,128)S(1)} fusion(f32[6,2,14336]{2,0,1:T(8,128)S(1)} %stack.4, f32[32]{0:T(128)S(1)} %get-tuple-element.350, f32[6,32]{1,0:T(8,128)S(1)} %get-tuple-element.349), kind=kOutput, calls=%fused_computation.2.clone.1 | convolution fusion | flops 67895296 | bytes 4359040 | tf_op jit(solution)/shard_map/while/body/eval_jaxpr/fh,fab->hab/dot_general | solution.py:56
  142.1 2.1 fusion.29
  148.3 3.2 %fusion.28 = f32[32,2,14336]{2,0,1:T(8,128)S(1)} fusion(f32[6,2,14336]{2,0,1:T(8,128)S(1)} %stack.4, f32[32]{0:T(128)S(1)} %get-tuple-element.350, f32[6,32]{1,0:T(8,128)S(1)} %get-tuple-element.349), kind=kOutput, calls=%fused_computation.2.clone.1 | convolution fusion | flops 67895296 | bytes 4359040 | tf_op jit(solution)/shard_map/while/body/eval_jaxpr/fh,fab->hab/dot_general | solution.py:56
  151.5 2.1 fusion.29
  157.8 3.2 %fusion.28 = f32[32,2,14336]{2,0,1:T(8,128)S(1)} fusion(f32[6,2,14336]{2,0,1:T(8,128)S(1)} %stack.4, f32[32]{0:T(128)S(1)} %get-tuple-element.350, f32[6,32]{1,0:T(8,128)S(1)} %get-tuple-element.349), kind=kOutput, calls=%fused_computation.2.clone.1 | convolution fusion | flops 67895296 | bytes 4359040 | tf_op jit(solution)/shard_map/while/body/eval_jaxpr/fh,fab->hab/dot_general | solution.py:56
  161.0 2.1 fusion.29
  164.0 2.0 broadcast_in_dim_reshape.3
  166.0 66.5 %all-gather.2.cloned.1.call-done = bf16[1,256,14336]{2,1,0:T(8,128)(2,1)} async-done(((bf16[1,16,14336]{2,1,0:T(8,128)(2,1)}), bf16[1,256,14336]{2,1,0:T(8,128)(2,1)}) %all-gather.2.cloned.1.call-update) | async-done | bytes 7340048 | tf_op jit(solution)/shard_map/all_gather | solution.py:116
  232.5 6.9 %copy.86 = bf16[1,256,14336]{2,1,0:T(8,128)(2,1)} copy(bf16[1,256,14336]{2,1,0:T(8,128)(2,1)} %all-gather.2.cloned.1.call-done) | data formatting | bytes 14680064
  (79 shorter events, 33.1 us)
Async XLA Ops:
  13.2 6.1 %copy-start.1 = (bf16[1,16,14336]{2,1,0:T(8,128)(2,1)S(1)}, bf16[1,16,14336]{2,1,0:T(8,128)(2,1)}, u32[]{:S(2)}) copy-start(bf16[1,16,14336]{2,1,0:T(8,128)(2,1)} %param.13) | copy-start | bytes 1376260
  13.3 49.3 %all-to-all-start = ((bf16[1,8,16,14336]{3,2,0,1:T(8,128)(2,1)}), bf16[1,8,16,14336]{3,2,0,1:T(8,128)(2,1)}, u32[]{:S(2)}, u32[]{:S(2)}) async-start(bf16[1,8,16,14336]{3,2,0,1:T(8,128)(2,1)} %multiply_convert_fusion), calls=%async_computation | async-start | bytes 7340032 | tf_op jit(solution)/shard_map/all_to_all | solution.py:78
  19.3 47.3 %copy-start = (f32[1,16,14336]{2,1,0:T(8,128)S(1)}, f32[1,16,14336]{2,1,0:T(8,128)}, u32[]{:S(2)}) copy-start(f32[1,16,14336]{2,1,0:T(8,128)} %param.14) | copy-start | bytes 2752516
  69.5 17.1 %all-to-all-start.1 = ((f32[16,1,2]{2,1,0:T(1,128)}), f32[16,1,2]{2,1,0:T(1,128)S(1)}, u32[]{:S(2)}, u32[]{:S(2)}) async-start(f32[16,1,2]{2,1,0:T(1,128)} %broadcast_in_dim.18), calls=%async_computation.1 | async-start | bytes 16384 | tf_op jit(solution)/shard_map/all_to_all | solution.py:16
  77.1 155.4 %all-gather.2.cloned.1.call-start = ((), (), s32[]{:S(2)}) async-start(), calls=%async_computation.2 | async-start | bytes 7798784 | tf_op jit(solution)/shard_map/all_gather | solution.py:116
  81.9 6.5 %copy-start.2 = (f32[6,32]{1,0:T(8,128)S(1)}, f32[6,32]{1,0:T(8,128)}, u32[]{:S(2)}) copy-start(f32[6,32]{1,0:T(8,128)} %param.16) | copy-start | bytes 2308
  81.9 6.5 %copy-start.3 = (f32[32,2]{0,1:T(2,128)S(1)}, f32[32,2]{0,1:T(2,128)}, u32[]{:S(2)}) copy-start(f32[32,2]{0,1:T(2,128)} %param.18) | copy-start | bytes 772
  81.9 6.5 %copy-start.4 = (f32[32]{0:T(128)S(1)}, f32[32]{0:T(128)}, u32[]{:S(2)}) copy-start(f32[32]{0:T(128)} %param.17) | copy-start | bytes 388
  81.9 6.5 %copy-start.5 = (f32[2]{0:T(128)S(1)}, f32[2]{0:T(128)}, u32[]{:S(2)}) copy-start(f32[2]{0:T(128)} %param.19) | copy-start | bytes 28
Sparse Core Ops, SparseCore 0:
  166.1 66.3 all-gather.1
where the time goes:
time: 247 us; the launch traced here: 246 us
  waiting for transfers between devices  109 us (44%)
  matrix products  42 us (17%)
  other arithmetic  35.8 us (14%)
  local copies, waits for them, and re-layouts  29.4 us (12%)
  between operations  15.4 us (6%)
  starting transfers between devices  13.9 us (6%)
    all_gather x1, waiting for transfers between devices, per_device(): gathered = lax.all_gather(updated[None], 'fs', axis=1, tiled=True)  66.5 us
    all_to_all x1, waiting for transfers between devices, per_device(): lax.all_to_all(outgoing, 'ep', split_axis=1, concat_axis=0, tiled=True)  42.8 us
    dot_general x8, matrix products, learned_step(): jnp.einsum('fh,fab->hab', in_weight, features, precision=lax.Precision.HI...  25.6 us
    dot_general x8, matrix products, learned_step(): jnp.einsum('hk,hab->kab', out_weight, hidden, precision=lax.Precision.HIG...  16.4 us
    mul x8, other arithmetic, learned_step(): gradient * inv_root  14.7 us
    another operation x8, local copies, waits for them, and re-layouts, learned_step(): jnp.stack([gradient / grad_norm, mom_next / mom_norm, mom_next * inv_root...  8.98 us
    all_to_all x1, starting transfers between devices, from_everyone(): return lax.all_to_all(copies, axis, split_axis=0, concat_axis=0, tiled=True)  7.6 us
    unnamed x13, local copies, waits for them, and re-layouts  6.93 us
  transfers between devices with their start and end apart: 3, of which 2 were waited for; matrix products, arithmetic and copies ran while one was open for 4% of the time, Pallas kernels for 0%

commit v1 on v0

--- a/solution.py
+++ b/solution.py
@@ -75,9 +75,12 @@
     share_row = lax.dynamic_index_in_dim(counts_f, source, 0, keepdims=False) / totals
     weighted = share_row[None, :, None, None] * grads.astype(jnp.float32)
     outgoing = weighted.astype(jnp.bfloat16)
-    gradient = add_sources(lax.all_to_all(outgoing, "ep", split_axis=1, concat_axis=0, tiled=True))[
-        0
-    ]
+    gradient = add_sources(
+        jnp.concatenate(
+            lax.all_to_all(jnp.stack(jnp.split(outgoing, lax.axis_size("ep"), axis=1)), "ep", 0, 0),
+            axis=0,
+        )
+    )[0]
     mom_here = mom[0]
     second_here = second[0]
     mom_next = MOMENTUM_DECAY * mom_here + (1.0 - MOMENTUM_DECAY) * gradient

time: 247 us -> 252 us (1.020)
  local copies, waits for them, and re-layouts: 29.4 us -> 35.8 us
    unnamed x13 -> x20, local copies, waits for them, and re-layouts: 6.93 us -> 12.5 us
where the time goes in v1:
time: 252 us; the launch traced here: 251 us
  waiting for transfers between devices  109 us (43%)
  matrix products  42 us (17%)
  local copies, waits for them, and re-layouts  35.8 us (14%)
  other arithmetic  33.9 us (13%)
  between operations  15.4 us (6%)
  starting transfers between devices  13.9 us (6%)
    all_gather x1, waiting for transfers between devices, per_device(): gathered = lax.all_gather(updated[None], 'fs', axis=1, tiled=True)  66.5 us
    all_to_all x1, waiting for transfers between devices, per_device(): lax.all_to_all(jnp.stack(jnp.split(outgoing, lax.axis_size('ep'), axis=1)...  42.8 us
    dot_general x8, matrix products, learned_step(): jnp.einsum('fh,fab->hab', in_weight, features, precision=lax.Precision.HI...  25.6 us
    dot_general x8, matrix products, learned_step(): jnp.einsum('hk,hab->kab', out_weight, hidden, precision=lax.Precision.HIG...  16.4 us
    mul x8, other arithmetic, learned_step(): gradient * inv_root  14.7 us
    unnamed x20, local copies, waits for them, and re-layouts  12.5 us
    another operation x8, local copies, waits for them, and re-layouts, learned_step(): jnp.stack([gradient / grad_norm, mom_next / mom_norm, mom_next * inv_root...  8.98 us
    all_to_all x1, starting transfers between devices, from_everyone(): return lax.all_to_all(copies, axis, split_axis=0, concat_axis=0, tiled=True)  7.6 us
  transfers between devices with their start and end apart: 3, of which 2 were waited for; matrix products, arithmetic and copies ran while one was open for 4% of the time, Pallas kernels for 0%

profile of v1, /device:TPU:1, one launch (start us, length us, event | category | flops | bytes accessed | tf_op | source)
XLA Modules:
  0.0 250.8 jit_solution(5318484901330291755)
XLA Ops:
  8.6 2.8 %multiply_convert_fusion = bf16[1,8,16,14336]{3,2,1,0:T(8,128)(2,1)S(1)} fusion(bf16[1,8,16,14336]{3,2,1,0:T(8,128)(2,1)} %param.11, f32[8]{0:T(128)S(1)} %bitcast_divide_fusion), kind=kLoop, calls=%fused_computation.22 | loop fusion | flops 5505024 | bytes 7340064 | tf_op jit(solution)/shard_map/convert_element_type | solution.py:77
  17.8 6.1 %all-to-all-start = ((bf16[8,1,1,16,14336]{4,3,2,1,0:T(8,128)(2,1)}), bf16[8,1,1,16,14336]{4,3,2,1,0:T(8,128)(2,1)}, u32[]{:S(2)}, u32[]{:S(2)}) async-start(bf16[8,1,1,16,14336]{4,3,2,1,0:T(8,128)(2,1)} %fusion.14), calls=%async_computation | async-start | bytes 7340032 | tf_op jit(solution)/shard_map/all_to_all | solution.py:80
  24.2 42.8 %all-to-all-done = bf16[8,1,1,16,14336]{4,3,2,1,0:T(8,128)(2,1)} async-done(((bf16[8,1,1,16,14336]{4,3,2,1,0:T(8,128)(2,1)}), bf16[8,1,1,16,14336]{4,3,2,1,0:T(8,128)(2,1)}, u32[]{:S(2)}, u32[]{:S(2)}) %all-to-all-start) | async-done | bytes 3670048 | tf_op jit(solution)/shard_map/all_to_all | solution.py:80
  67.0 2.6 %convert_reduce_fusion = f32[16,14336]{1,0:T(8,128)S(1)} fusion(bf16[8,1,1,16,14336]{4,3,2,1,0:T(8,128)(2,1)} %all-to-all-done), kind=kLoop, calls=%fused_computation.21 | loop fusion | flops 3440640 | bytes 4587520 | tf_op jit(solution)/shard_map/reduce_sum | solution.py:68
  74.0 7.6 %all-to-all-start.1 = ((f32[16,1,2]{2,1,0:T(1,128)}), f32[16,1,2]{2,1,0:T(1,128)S(1)}, u32[]{:S(2)}, u32[]{:S(2)}) async-start(f32[16,1,2]{2,1,0:T(1,128)} %broadcast_in_dim.18), calls=%async_computation.1 | async-start | bytes 16384 | tf_op jit(solution)/shard_map/all_to_all | solution.py:16
  81.8 2.9 %fusion.10 = (f32[1,16,14336]{2,1,0:T(8,128)}, f32[1,16,14336]{2,1,0:T(8,128)}, f32[1,16,14336]{2,1,0:T(8,128)}, f32[1,16,14336]{2,1,0:T(8,128)S(1)}) fusion(f32[16,14336]{1,0:T(8,128)S(1)} %convert_reduce_fusion, f32[1,16,14336]{2,1,0:T(8,128)} %param.15, f32[1,16,14336]{2,1,0:T(8,128)S(1)} %copy-done), kind=kLoop, calls=%fused_computation.26 | loop fusion | flops 1605632 | bytes 6422528 | tf_op jit(solution)/shard_map/add | solution.py:87
  87.0 4.1 %fusion.9 = (f32[8,2,14336]{2,0,1:T(8,128)S(1)}, f32[8,2,14336]{2,0,1:T(8,128)}, f32[8,2,14336]{2,0,1:T(8,128)}) fusion(f32[8,2,14336]{2,1,0:T(2,128)S(1)} %mul.131, f32[8,2,14336]{2,1,0:T(2,128)} %reshape_squeeze.7, f32[8,2,14336]{2,1,0:T(2,128)S(1)} %mul.126), kind=kLoop, calls=%fused_computation.25 | loop fusion | flops 1146880 | bytes 5505024 | tf_op jit(solution)/shard_map/add | solution.py:87
  93.0 75.6 %while.11 = (s32[]{:T(128)}, bf16[8,2,14336]{2,1,0:T(2,128)(2,1)}, bf16[8,2,14336]{2,1,0:T(2,128)(2,1)S(1)}, f32[8,2,14336]{2,0,1:T(8,128)}, f32[]{:T(128)}, /*i...) while((s32[]{:T(128)}, bf16[8,2,14336]{2,1,0:T(2,128)(2,1)}, ...), condition=%wide.region_6.7_spmd, body=%wide.region_5.6_spmd.sunk | while | flops 90316800 | bytes 11298093 | solution.py:109
  93.2 1.8 dynamic-slice_multiply_fusion.3
  96.2 3.2 %fusion.36 = f32[32,2,14336]{2,0,1:T(8,128)S(1)} fusion(f32[6,2,14336]{2,0,1:T(8,128)S(1)} %stack.46, f32[32]{0:T(128)S(1)} %get-tuple-element.337, f32[6,32]{1,0:T(8,128)S(1)} %get-tuple-element.336), kind=kOutput, calls=%fused_computation.2.clone.1 | convolution fusion | flops 67895296 | bytes 4359040 | tf_op jit(solution)/shard_map/while/body/eval_jaxpr/fh,fab->hab/dot_general | solution.py:56
  99.4 2.1 fusion.37
  102.6 1.8 dynamic-slice_multiply_fusion.3
  105.6 3.2 %fusion.36 = f32[32,2,14336]{2,0,1:T(8,128)S(1)} fusion(f32[6,2,14336]{2,0,1:T(8,128)S(1)} %stack.46, f32[32]{0:T(128)S(1)} %get-tuple-element.337, f32[6,32]{1,0:T(8,128)S(1)} %get-tuple-element.336), kind=kOutput, calls=%fused_computation.2.clone.1 | convolution fusion | flops 67895296 | bytes 4359040 | tf_op jit(solution)/shard_map/while/body/eval_jaxpr/fh,fab->hab/dot_general | solution.py:56
  108.8 2.1 fusion.37
  112.1 1.8 dynamic-slice_multiply_fusion.3
  115.1 3.2 %fusion.36 = f32[32,2,14336]{2,0,1:T(8,128)S(1)} fusion(f32[6,2,14336]{2,0,1:T(8,128)S(1)} %stack.46, f32[32]{0:T(128)S(1)} %get-tuple-element.337, f32[6,32]{1,0:T(8,128)S(1)} %get-tuple-element.336), kind=kOutput, calls=%fused_computation.2.clone.1 | convolution fusion | flops 67895296 | bytes 4359040 | tf_op jit(solution)/shard_map/while/body/eval_jaxpr/fh,fab->hab/dot_general | solution.py:56
  118.3 2.1 fusion.37
  121.5 1.8 dynamic-slice_multiply_fusion.3
  124.5 3.2 %fusion.36 = f32[32,2,14336]{2,0,1:T(8,128)S(1)} fusion(f32[6,2,14336]{2,0,1:T(8,128)S(1)} %stack.46, f32[32]{0:T(128)S(1)} %get-tuple-element.337, f32[6,32]{1,0:T(8,128)S(1)} %get-tuple-element.336), kind=kOutput, calls=%fused_computation.2.clone.1 | convolution fusion | flops 67895296 | bytes 4359040 | tf_op jit(solution)/shard_map/while/body/eval_jaxpr/fh,fab->hab/dot_general | solution.py:56
  127.7 2.1 fusion.37
  131.0 1.8 dynamic-slice_multiply_fusion.3
  134.0 3.2 %fusion.36 = f32[32,2,14336]{2,0,1:T(8,128)S(1)} fusion(f32[6,2,14336]{2,0,1:T(8,128)S(1)} %stack.46, f32[32]{0:T(128)S(1)} %get-tuple-element.337, f32[6,32]{1,0:T(8,128)S(1)} %get-tuple-element.336), kind=kOutput, calls=%fused_computation.2.clone.1 | convolution fusion | flops 67895296 | bytes 4359040 | tf_op jit(solution)/shard_map/while/body/eval_jaxpr/fh,fab->hab/dot_general | solution.py:56
  137.2 2.1 fusion.37
  143.4 3.2 %fusion.36 = f32[32,2,14336]{2,0,1:T(8,128)S(1)} fusion(f32[6,2,14336]{2,0,1:T(8,128)S(1)} %stack.46, f32[32]{0:T(128)S(1)} %get-tuple-element.337, f32[6,32]{1,0:T(8,128)S(1)} %get-tuple-element.336), kind=kOutput, calls=%fused_computation.2.clone.1 | convolution fusion | flops 67895296 | bytes 4359040 | tf_op jit(solution)/shard_map/while/body/eval_jaxpr/fh,fab->hab/dot_general | solution.py:56
  146.6 2.1 fusion.37
  152.8 3.2 %fusion.36 = f32[32,2,14336]{2,0,1:T(8,128)S(1)} fusion(f32[6,2,14336]{2,0,1:T(8,128)S(1)} %stack.46, f32[32]{0:T(128)S(1)} %get-tuple-element.337, f32[6,32]{1,0:T(8,128)S(1)} %get-tuple-element.336), kind=kOutput, calls=%fused_computation.2.clone.1 | convolution fusion | flops 67895296 | bytes 4359040 | tf_op jit(solution)/shard_map/while/body/eval_jaxpr/fh,fab->hab/dot_general | solution.py:56
  156.1 2.1 fusion.37
  162.3 3.2 %fusion.36 = f32[32,2,14336]{2,0,1:T(8,128)S(1)} fusion(f32[6,2,14336]{2,0,1:T(8,128)S(1)} %stack.46, f32[32]{0:T(128)S(1)} %get-tuple-element.337, f32[6,32]{1,0:T(8,128)S(1)} %get-tuple-element.336), kind=kOutput, calls=%fused_computation.2.clone.1 | convolution fusion | flops 67895296 | bytes 4359040 | tf_op jit(solution)/shard_map/while/body/eval_jaxpr/fh,fab->hab/dot_general | solution.py:56
  165.5 2.1 fusion.37
  168.6 2.0 broadcast_in_dim_reshape.3
  170.5 66.5 %all-gather.2.cloned.1.call-done = bf16[1,256,14336]{2,1,0:T(8,128)(2,1)} async-done(((bf16[1,16,14336]{2,1,0:T(8,128)(2,1)}), bf16[1,256,14336]{2,1,0:T(8,128)(2,1)}) %all-gather.2.cloned.1.call-update) | async-done | bytes 7340048 | tf_op jit(solution)/shard_map/all_gather | solution.py:119
  237.0 6.9 %copy.82 = bf16[1,256,14336]{2,1,0:T(8,128)(2,1)} copy(bf16[1,256,14336]{2,1,0:T(8,128)(2,1)} %all-gather.2.cloned.1.call-done) | data formatting | bytes 14680064
  (87 shorter events, 39.5 us)
Async XLA Ops:
  17.8 6.1 %copy-start.1 = (bf16[1,16,14336]{2,1,0:T(8,128)(2,1)S(1)}, bf16[1,16,14336]{2,1,0:T(8,128)(2,1)}, u32[]{:S(2)}) copy-start(bf16[1,16,14336]{2,1,0:T(8,128)(2,1)} %param.13) | copy-start | bytes 1376260
  17.8 49.3 %all-to-all-start = ((bf16[8,1,1,16,14336]{4,3,2,1,0:T(8,128)(2,1)}), bf16[8,1,1,16,14336]{4,3,2,1,0:T(8,128)(2,1)}, u32[]{:S(2)}, u32[]{:S(2)}) async-start(bf16[8,1,1,16,14336]{4,3,2,1,0:T(8,128)(2,1)} %fusion.14), calls=%async_computation | async-start | bytes 7340032 | tf_op jit(solution)/shard_map/all_to_all | solution.py:80
  23.9 47.3 %copy-start = (f32[1,16,14336]{2,1,0:T(8,128)S(1)}, f32[1,16,14336]{2,1,0:T(8,128)}, u32[]{:S(2)}) copy-start(f32[1,16,14336]{2,1,0:T(8,128)} %param.14) | copy-start | bytes 2752516
  74.0 17.1 %all-to-all-start.1 = ((f32[16,1,2]{2,1,0:T(1,128)}), f32[16,1,2]{2,1,0:T(1,128)S(1)}, u32[]{:S(2)}, u32[]{:S(2)}) async-start(f32[16,1,2]{2,1,0:T(1,128)} %broadcast_in_dim.18), calls=%async_computation.1 | async-start | bytes 16384 | tf_op jit(solution)/shard_map/all_to_all | solution.py:16
  81.6 155.4 %all-gather.2.cloned.1.call-start = ((), (), s32[]{:S(2)}) async-start(), calls=%async_computation.2 | async-start | bytes 7798784 | tf_op jit(solution)/shard_map/all_gather | solution.py:119
  86.4 6.5 %copy-start.2 = (f32[6,32]{1,0:T(8,128)S(1)}, f32[6,32]{1,0:T(8,128)}, u32[]{:S(2)}) copy-start(f32[6,32]{1,0:T(8,128)} %param.16) | copy-start | bytes 2308
  86.4 6.5 %copy-start.3 = (f32[32,2]{0,1:T(2,128)S(1)}, f32[32,2]{0,1:T(2,128)}, u32[]{:S(2)}) copy-start(f32[32,2]{0,1:T(2,128)} %param.18) | copy-start | bytes 772
  86.4 6.5 %copy-start.4 = (f32[32]{0:T(128)S(1)}, f32[32]{0:T(128)}, u32[]{:S(2)}) copy-start(f32[32]{0:T(128)} %param.17) | copy-start | bytes 388
  86.5 6.5 %copy-start.5 = (f32[2]{0:T(128)S(1)}, f32[2]{0:T(128)}, u32[]{:S(2)}) copy-start(f32[2]{0:T(128)} %param.19) | copy-start | bytes 28
Sparse Core Ops, SparseCore 0:
  170.7 66.3 all-gather.1
